TPU v7x, 32 devices: a whole 2x2x4 slice. The times are simulated.
32 devices in a mesh: prompts: 2 (over x), model: 4 (over z), resp: 4 (over y, core).
Axes of the slice: x: 2, y: 2, z: 4, core: 2. Of those that a mesh axis runs over, the one named last changes fastest.
Arguments:
- x_prompt: bfloat16 [4096, 2560], P(('prompts', 'resp')), parts along dimension 0
- x_resp: bfloat16 [8, 1024, 2560], P(('prompts', 'resp')), parts along dimension 0
- targets: int32 [8, 1024], P(('prompts', 'resp')), parts along dimension 0
- resp_lens: int32 [8], P(('prompts', 'resp')), parts along dimension 0
- attn_gain: float32 [2, 2560], replicated
- w_query: bfloat16 [2, 2560, 20, 128], P(None, None, 'model')
- w_key: bfloat16 [2, 2560, 20, 128], P(None, None, 'model')
- w_value: bfloat16 [2, 2560, 20, 128], P(None, None, 'model')
- w_out: bfloat16 [2, 20, 128, 2560], P(None, 'model')
- mlp_gain: float32 [2, 2560], replicated
- w_gate: bfloat16 [2, 2560, 6912], P(None, None, 'model')
- w_up: bfloat16 [2, 2560, 6912], P(None, None, 'model')
- w_down: bfloat16 [2, 6912, 2560], P(None, 'model')
- final_gain: float32 [2560], replicated
- w_vocab: bfloat16 [2560, 65536], P(None, 'model')
Outputs:
- output: float32 [8, 1024], P(('prompts', 'resp')), parts along dimension 0
There are 2 independent parts. A program takes and returns all parts, laid end to end along the dimension named above; an argument that names none is the same for every part.
All inputs are finite; a program needn't handle non-finite values.
Results may differ from a plain program's by a relative error of at most 0.00229753.
Values are sent between devices in bfloat16 or wider.
A program may use at most 1 GiB of HBM per device.

v0:
```python
import jax
import jax.numpy as jnp
from jax import lax
from jax.sharding import PartitionSpec as P

EPS = 1e-6
ROPE_BASE = 10000.0


def rms_norm(acts_in, gain_vec):
    acts_f = acts_in.astype(jnp.float32)
    inv_rms = lax.rsqrt(jnp.mean(acts_f * acts_f, axis=-1, keepdims=True) + EPS)
    return (acts_f * inv_rms * gain_vec).astype(jnp.bfloat16)


def rotary(projected, positions):
    half_dim = projected.shape[-1] // 2
    frequency = ROPE_BASE ** (-jnp.arange(half_dim, dtype=jnp.float32) / half_dim)
    angles = positions.astype(jnp.float32)[..., None] * frequency
    cos_part = jnp.cos(angles)[..., None, :]
    sin_part = jnp.sin(angles)[..., None, :]
    lower_half = projected[..., :half_dim]
    upper_half = projected[..., half_dim:]
    return jnp.concatenate([lower_half * cos_part - upper_half * sin_part, upper_half * cos_part + lower_half * sin_part], axis=-1)


def attend(queries, keys, values, query_pos, key_pos):
    heads, head_dim = queries.shape[-2], queries.shape[-1]
    kv_heads = keys.shape[-2]
    grouped = queries.reshape(queries.shape[:-2] + (kv_heads, heads // kv_heads, head_dim))
    scores = jnp.einsum('...tkrd,...skd->...krts', grouped, keys, preferred_element_type=jnp.float32) * (head_dim ** -0.5)
    visible = (key_pos[None, :] <= query_pos[..., :, None])[..., None, None, :, :]
    scores = jnp.where(visible, scores, -jnp.inf)
    row_max = jnp.max(scores, axis=-1, keepdims=True)
    exp_scores = jnp.exp(scores - row_max)
    row_sum = jnp.moveaxis(jnp.sum(exp_scores, axis=-1), -1, -3)
    mixed = jnp.einsum('...krts,...skd->...tkrd', exp_scores.astype(jnp.bfloat16), values, preferred_element_type=jnp.float32)
    return (mixed / row_sum[..., None]).reshape(queries.shape).astype(jnp.bfloat16)


def solution(mesh):
    groups = mesh.shape['resp']
    row_axes = ('prompts', 'resp')
    head_spec = P(None, None, 'model', None)
    in_specs = (P(row_axes, None), P(row_axes, None, None), P(row_axes, None), P(row_axes), P(None, None), head_spec, head_spec, head_spec, P(None, 'model', None, None), P(None, None), P(None, None, 'model'), P(None, None, 'model'), P(None, 'model', None), P(None), P(None, 'model'))

    def device_step(x_prompt, x_resp, targets, resp_lens, attn_gain, w_query, w_key, w_value, w_out, mlp_gain, w_gate, w_up, w_down, final_gain, w_vocab):
        prompt_rows = x_prompt.shape[0]
        resp_len = x_resp.shape[1]
        prompt_len = prompt_rows * groups
        num_layers = w_query.shape[0]
        resp_pos = prompt_len + jnp.arange(resp_len)
        tok_pos = jnp.concatenate([lax.axis_index('resp') * prompt_rows + jnp.arange(prompt_rows), resp_pos])
        key_pos = jnp.concatenate([jnp.arange(prompt_len), resp_pos])
        residual = jnp.concatenate([x_prompt, x_resp[0]], axis=0)
        for layer_idx in range(num_layers):
            hidden = rms_norm(residual, attn_gain[layer_idx])
            keys = rotary(jnp.einsum('td,dhe->the', hidden, w_key[layer_idx], preferred_element_type=jnp.float32), tok_pos).astype(jnp.bfloat16)
            values = jnp.einsum('td,dhe->the', hidden, w_value[layer_idx], preferred_element_type=jnp.float32).astype(jnp.bfloat16)
            prompt_keys = lax.all_gather(keys[:prompt_rows], 'resp', axis=0, tiled=True)
            prompt_values = lax.all_gather(values[:prompt_rows], 'resp', axis=0, tiled=True)
            all_keys = jnp.concatenate([prompt_keys, keys[prompt_rows:]], axis=0)
            all_values = jnp.concatenate([prompt_values, values[prompt_rows:]], axis=0)
            query_pos = tok_pos
            if layer_idx == num_layers - 1:
                residual = residual[prompt_rows:]
                hidden = hidden[prompt_rows:]
                query_pos = resp_pos
            queries = rotary(jnp.einsum('td,dhe->the', hidden, w_query[layer_idx], preferred_element_type=jnp.float32), query_pos).astype(jnp.bfloat16)
            mixed = attend(queries, all_keys, all_values, query_pos, key_pos)
            attn_part = jnp.einsum('the,hed->td', mixed, w_out[layer_idx], preferred_element_type=jnp.float32)
            residual = (residual.astype(jnp.float32) + lax.psum(attn_part, 'model')).astype(jnp.bfloat16)
            hidden = rms_norm(residual, mlp_gain[layer_idx])
            gate = jnp.dot(hidden, w_gate[layer_idx], preferred_element_type=jnp.float32)
            up_proj = jnp.dot(hidden, w_up[layer_idx], preferred_element_type=jnp.float32)
            inner = (jax.nn.silu(gate) * up_proj).astype(jnp.bfloat16)
            down_part = jnp.dot(inner, w_down[layer_idx], preferred_element_type=jnp.float32)
            residual = (residual.astype(jnp.float32) + lax.psum(down_part, 'model')).astype(jnp.bfloat16)
        logits = jnp.dot(rms_norm(residual, final_gain), w_vocab, preferred_element_type=jnp.float32)
        vocab_local = logits.shape[-1]
        vocab_ids = lax.axis_index('model') * vocab_local + jnp.arange(vocab_local)
        row_max = lax.pmax(jnp.max(logits, axis=-1), 'model')
        exp_total = lax.psum(jnp.sum(jnp.exp(logits - row_max[:, None]), axis=-1), 'model')
        picked = lax.psum(jnp.sum(jnp.where(vocab_ids[None, :] == targets[0][:, None], logits, 0.0), axis=-1), 'model')
        log_probs = picked - row_max - jnp.log(exp_total)
        log_probs = jnp.where(jnp.arange(resp_len) < resp_lens[0], log_probs, 0.0)
        return log_probs[None, :]

    return jax.shard_map(device_step, mesh=mesh, in_specs=in_specs, out_specs=P(row_axes, None), check_vma=False)
```

profile of v0, /device:TPU:0, one launch (start us, length us, event | category | flops | bytes accessed | tf_op | source)
XLA Modules:
  0.0 2401.3 jit_solution(9641396961747860258)
XLA Ops:
  18.4 6.3 fusion.155
  30.4 7.7 fusion.19
  53.5 9.7 fusion.102
  71.1 10.5 all-gather.7.cloned.1.call-done
  81.6 36.8 %fusion.2 = (f32[5,1536]{1,0:T(8,128)S(1)}, f32[5,3072,1536]{2,1,0:T(8,128)}) fusion(pred[1536,3072]{0,1:T(8,128)(4,1)} %broadcast_compare_fusion, bf16[1536,5,64]{0,2,1:T(8,128)(2,1)} %get-tuple-element.26, bf16[1536,5,64]{0,2,1:T(8,128)(2,1)S(1)} %get-tuple-element.25, bf16[1536,5,64]{0,2,1:T(8,128)(2,1)S(1)} %get-tuple-element.31, ...), kind=kOutput, calls=%fused_computation.4 | convolution fusion | flops 6132195840 | bytes 105674752 | tf_op jit(solution)/shard_map/...tkrd,...skd->...krts/dot_general | solution.py:31
  118.4 30.8 %fusion = f32[5,1536]{1,0:T(8,128)S(1)} fusion(f32[5,3072,1536]{2,1,0:T(8,128)} %get-tuple-element.40, f32[5,1536]{1,0:T(8,128)S(1)} %get-tuple-element.39, pred[1536,3072]{0,1:T(8,128)(4,1)} %broadcast_compare_fusion), kind=kLoop, calls=%fused_computation.2 | loop fusion | flops 94364160 | bytes 99151872 | tf_op jit(solution)/shard_map/reduce_sum | solution.py:36
  149.3 39.6 %fusion.112 = bf16[1536,5,128]{0,2,1:T(8,128)(2,1)} fusion(f32[5,3072,1536]{2,1,0:T(8,128)} %get-tuple-element.40, f32[5,1536]{1,0:T(8,128)S(1)} %get-tuple-element.39, pred[1536,3072]{0,1:T(8,128)(4,1)} %broadcast_compare_fusion, bf16[1024,5,128]{2,0,1:T(8,128)(2,1)S(1)} %slice-done, bf16[2048,5,128]{2,0,1:T(8,128)(2,1)} %all-gather.5.cloned.1.call-done, ...), kind=kOutput, calls=%fused_computation.120 | convolution fusion | flops 6144000000 | bytes 105050112 | tf_op jit(solution)/shard_map/...krts,...skd->...tkrd/dot_general | solution.py:37
  188.9 12.0 convolution_bitcast_fusion
  202.2 524.7 %all-reduce.6.cloned.1.call-done = f32[1536,2560]{1,0:T(8,128)} async-done(((f32[1536,2560]{1,0:T(8,128)}), f32[1536,2560]{1,0:T(8,128)}) %all-reduce.6.cloned.1.call-update) | async-done | bytes 15728656 | tf_op jit(solution)/shard_map/psum | solution.py:72
  726.9 8.3 fusion.21
  735.3 20.5 fusion.41
  755.8 18.0 multiply_convert_fusion
  773.8 20.7 fusion.38
  799.9 519.4 %all-reduce.8.cloned.1.call-done = f32[1536,2560]{1,0:T(8,128)} async-done(((f32[1536,2560]{1,0:T(8,128)}), f32[1536,2560]{1,0:T(8,128)}) %all-reduce.8.cloned.1.call-update) | async-done | bytes 15728656 | tf_op jit(solution)/shard_map/psum | solution.py:78
  1319.4 8.8 fusion.14
  1333.6 8.7 fusion.159
  1352.5 9.6 fusion.107
  1366.8 8.7 fusion.59
  1378.8 26.6 %fusion.5 = (f32[5,1024]{1,0:T(8,128)S(1)}, f32[5,3072,1024]{2,1,0:T(8,128)}) fusion(pred[1024,3072]{0,1:T(8,128)(4,1)S(1)} %broadcast_compare_fusion.1, bf16[1024,5,64]{0,2,1:T(8,128)(2,1)} %get-tuple-element.30, bf16[1024,5,64]{0,2,1:T(8,128)(2,1)} %get-tuple-element.29, bf16[1536,5,64]{0,2,1:T(8,128)(2,1)} %copy-done.9, ...), kind=kOutput, calls=%fused_computation.11 | convolution fusion | flops 4094028800 | bytes 71979008 | tf_op jit(solution)/shard_map/...tkrd,...skd->...krts/dot_general | solution.py:31
  1405.4 20.3 fusion.3
  1425.7 26.8 %fusion.131 = bf16[1024,5,128]{0,2,1:T(8,128)(2,1)} fusion(f32[5,3072,1024]{2,1,0:T(8,128)} %get-tuple-element.42, f32[5,1024]{1,0:T(8,128)S(1)} %get-tuple-element.41, pred[1024,3072]{0,1:T(8,128)(4,1)S(1)} %broadcast_compare_fusion.1, bf16[1024,5,128]{2,0,1:T(8,128)(2,1)} %slice.152, bf16[2048,5,128]{2,0,1:T(8,128)(2,1)} %all-gather.9.cloned.1.call-done, ...), kind=kOutput, calls=%fused_computation.134 | convolution fusion | flops 4098621440 | bytes 71344128 | tf_op jit(solution)/shard_map/...krts,...skd->...tkrd/dot_general | solution.py:37
  1452.5 10.4 convolution_bitcast_fusion.1
  1463.1 355.4 %all-reduce.10.cloned.1.call-done = f32[1024,2560]{1,0:T(8,128)} async-done(((f32[1024,2560]{1,0:T(8,128)}), f32[1024,2560]{1,0:T(8,128)}) %all-reduce.10.cloned.1.call-update) | async-done | bytes 10485776 | tf_op jit(solution)/shard_map/psum | solution.py:72
  1818.5 9.8 fusion.28
  1828.3 15.5 fusion.34
  1843.8 46.3 %fusion.32 = f32[1024,2560]{1,0:T(8,128)} fusion(bf16[2,1728,2560]{2,1,0:T(8,128)(2,1)} %param.27, f32[1024,1728]{0,1:T(8,128)} %fusion.34, bf16[2,2560,1728]{1,2,0:T(8,128)(2,1)} %param.25, bf16[1024,2560]{1,0:T(8,128)(2,1)} %get-tuple-element.14, f32[2560]{0:T(1024)S(1)} %copy-done.26, f32[1024]{0:T(1024)S(1)} %add_rsqrt_fusion.4), kind=kOutput, calls=%fused_computation.53 | convolution fusion | flops 18140495872 | bytes 40515584 | tf_op jit(solution)/shard_map/dot_general | solution.py:77
  1891.4 354.3 %all-reduce.12.cloned.1.call-done = f32[1024,2560]{1,0:T(8,128)} async-done(((f32[1024,2560]{1,0:T(8,128)}), f32[1024,2560]{1,0:T(8,128)}) %all-reduce.12.cloned.1.call-update) | async-done | bytes 10485776 | tf_op jit(solution)/shard_map/psum | solution.py:78
  2245.7 6.9 fusion.25
  2252.7 100.5 %fusion.156 = (f32[1024]{0:T(1024)S(1)}, f32[1024,16384]{1,0:T(8,128)}) fusion(bf16[2560,16384]{1,0:T(8,128)(2,1)} %param.29, f32[2560]{0:T(1024)S(1)} %copy-done.30, f32[1024]{0:T(1024)S(1)} %add_rsqrt_fusion.3, f32[1024,2560]{1,0:T(8,128)} %all-reduce.12.cloned.1.call-done, bf16[1024,2560]{1,0:T(8,128)(2,1)} %get-tuple-element.14), kind=kOutput, calls=%fused_computation.177 | convolution fusion | flops 85934473216 | bytes 166742016 | tf_op jit(solution)/shard_map/dot_general | solution.py:79
  2353.1 9.9 pmax.7
  2363.1 21.6 select_reduce_fusion
  2384.7 9.0 all-reduce
  (120 shorter events, 72.2 us)
Async XLA Ops:
  6.5 5.1 copy-start.24
  6.5 75.1 %all-gather.7.cloned.1.call-start = ((), (), s32[]{:S(2)}) async-start(), calls=%async_computation.1 | async-start | bytes 3276800 | tf_op jit(solution)/shard_map/all_gather | solution.py:60
  6.5 42.1 %copy-start.28 = (f32[64]{0:T(128)}, f32[64]{0:T(128)S(1)}, u32[]{:S(2)}) copy-start(f32[64]{0:T(128)S(1)} %multiply_power_fusion) | copy-start | bytes 772
  6.6 59.0 %copy-start.21 = (s32[1024]{0:T(1024)}, s32[1024]{0:T(1024)S(1)}, u32[]{:S(2)}) copy-start(s32[1024]{0:T(1024)S(1)} %iota_add_fusion.1) | copy-start | bytes 12292
  6.6 5.7 copy-start.7
  18.4 12.0 copy-start.2
  30.4 7.7 copy-start.14
  38.0 5.3 copy-start.6
  38.0 5.3 copy-start.15
  50.1 2.4 copy-start.10
  53.5 95.8 %all-gather.5.cloned.1.call-start = ((), (), s32[]{:S(2)}) async-start(), calls=%async_computation | async-start | bytes 3276800 | tf_op jit(solution)/shard_map/all_gather | solution.py:61
  65.5 661.4 %all-reduce.6.cloned.1.call-start = ((), (), s32[]{:S(2)}) async-start(), calls=%async_computation.2 | async-start | bytes 31457280 | tf_op jit(solution)/shard_map/psum | solution.py:72
  118.4 30.9 %slice-start = ((bf16[1536,5,128]{2,0,1:T(8,128)(2,1)}), bf16[1024,5,128]{2,0,1:T(8,128)(2,1)S(1)}, s32[]{:S(2)}) async-start(bf16[1536,5,128]{2,0,1:T(8,128)(2,1)} %copy-done.16), calls=%async_computation.8 | async-start | bytes 2621440 | tf_op jit(solution)/shard_map/slice | solution.py:63
  200.8 526.1 %copy-start.3 = (bf16[512,2560]{1,0:T(8,128)(2,1)S(1)}, bf16[512,2560]{1,0:T(8,128)(2,1)}, u32[]{:S(2)}) copy-start(bf16[512,2560]{1,0:T(8,128)(2,1)} %param.15) | copy-start | bytes 7864324
  200.9 1118.5 %all-reduce.8.cloned.1.call-start = ((), (), s32[]{:S(2)}) async-start(), calls=%async_computation.3 | async-start | bytes 31457280 | tf_op jit(solution)/shard_map/psum | solution.py:78
  735.3 20.5 copy-start.1
  794.5 584.3 %all-gather.11.cloned.1.call-start = ((), (), s32[]{:S(2)}) async-start(), calls=%async_computation.5 | async-start | bytes 3276800 | tf_op jit(solution)/shard_map/all_gather | solution.py:60
  799.9 528.3 %copy-start.23 = (f32[2560]{0:T(1024)S(1)}, f32[2560]{0:T(1024)}, u32[]{:S(2)}) copy-start(f32[2560]{0:T(1024)} %get-tuple-element.9) | copy-start | bytes 30724
  1328.2 5.4 copy-start
  1333.6 8.7 copy-start.11
  1333.6 8.7 copy-start.13
  1342.3 3.0 copy-start.4
  1342.3 6.4 copy-start.29
  1342.3 8.1 copy-start.20
  1342.3 8.1 copy-start.22
  1345.2 80.5 %all-gather.9.cloned.1.call-start = ((), (), s32[]{:S(2)}) async-start(), calls=%async_computation.4 | async-start | bytes 3276800 | tf_op jit(solution)/shard_map/all_gather | solution.py:61
  1375.5 443.0 %all-reduce.10.cloned.1.call-start = ((), (), s32[]{:S(2)}) async-start(), calls=%async_computation.6 | async-start | bytes 20971520 | tf_op jit(solution)/shard_map/psum | solution.py:72
  1463.0 365.3 %copy-start.26 = (f32[2560]{0:T(1024)S(1)}, f32[2560]{0:T(1024)}, u32[]{:S(2)}) copy-start(f32[2560]{0:T(1024)} %get-tuple-element.7) | copy-start | bytes 30724
  1463.0 782.7 %all-reduce.12.cloned.1.call-start = ((), (), s32[]{:S(2)}) async-start(), calls=%async_computation.7 | async-start | bytes 20971520 | tf_op jit(solution)/shard_map/psum | solution.py:78
  1891.4 361.2 %copy-start.30 = (f32[2560]{0:T(1024)S(1)}, f32[2560]{0:T(1024)}, u32[]{:S(2)}) copy-start(f32[2560]{0:T(1024)} %param.28) | copy-start | bytes 30724
  2252.6 110.4 %copy-start.18 = (s32[16384]{0:T(1024)S(1)}, s32[16384]{0:T(1024)}, u32[]{:S(2)}) copy-start(s32[16384]{0:T(1024)} %iota_add_fusion) | copy-start | bytes 196612
  2252.7 110.4 %copy-start.27 = (s32[1,1024]{1,0:T(1,128)S(1)}, s32[1,1024]{1,0:T(1,128)}, u32[]{:S(2)}) copy-start(s32[1,1024]{1,0:T(1,128)} %param.17) | copy-start | bytes 12292
  (8 other events, 10.5 us)
Sparse Core Ops, SparseCore 0:
  53.6 27.9 all-gather.6
  83.2 25.1 all-gather.4
  201.0 525.8 all-reduce.5
  794.6 524.7 all-reduce.7
  1345.3 24.0 all-gather.10
  1375.6 24.0 all-gather.8
  1463.1 355.3 all-reduce.9
  1890.3 355.4 all-reduce.11
where the time goes:
time: 2400 us
  waiting for transfers between devices  1760 us (73%)
  matrix products  421 us (18%)
  other arithmetic  144 us (6%)
  local copies, waits for them, and re-layouts  37.7 us (2%)
    psum x2, waiting for transfers between devices, device_step(): lax.psum(attn_part, 'model')  880 us
    psum x2, waiting for transfers between devices, device_step(): lax.psum(down_part, 'model')  874 us
    dot_general x1, matrix products, device_step(): jnp.dot(rms_norm(residual, final_gain), w_vocab, preferred_element_type=j...  100 us
    dot_general x2, matrix products, device_step(): jnp.dot(inner, w_down[layer_idx], preferred_element_type=jnp.float32)  67 us
    dot_general x2, matrix products, attend(): jnp.einsum('...krts,...skd->...tkrd', exp_scores.astype(jnp.bfloat16), va...  66.4 us
    dot_general x2, matrix products, attend(): jnp.einsum('...tkrd,...skd->...krts', grouped, keys, preferred_element_ty...  63.4 us
    reduce_sum x2, other arithmetic, attend(): row_sum = jnp.moveaxis(jnp.sum(exp_scores, axis=-1), -1, -3)  51.2 us
  transfers between devices with their start and end apart: 8, of which 5 were waited for; matrix products, arithmetic and copies ran while one was open for 7% of the time, Pallas kernels for 0%

commit v1 on v0

v1 whole, which is shorter than its diff:
```python
import functools

import jax
import jax.numpy as jnp
from jax import lax
from jax.experimental import pallas as pl
from jax.experimental.pallas import tpu as pltpu
from jax.sharding import PartitionSpec as P

EPS = 1e-6
ROPE_BASE = 10000.0
LOG2E = 1.4426950408889634
HD = 128
NH = 5
NEG = -1e30
BF, F32 = jnp.bfloat16, jnp.float32
ANY = pl.BlockSpec(memory_space=pl.ANY)
VMEM = pl.BlockSpec(memory_space=pltpu.VMEM)
DMA = pltpu.SemaphoreType.DMA
MESH = pl.DeviceIdType.MESH
NT = (((1,), (1,)), ((), ()))


PLAN = (
    "z0000Q00/k0000z0001Q02/z0002Q01/k0001z0003x0000k0002A00/o000",
    "0A01/x0001o0001o0100A02/x0002o0002z1000o0101o0200x0003o0003T",
    "00/s0000z1001s0010o0102o0201z1002s0001s0011o0103T01/s0002s00",
    "12z1003x1000s0100o0202s0110s0101x1001s0003g0000s0013g0010s01",
    "11o0203T02/g0001g0011x1002s0102s0112s0200g0002x1003s0210g001",
    "2s0103g0100s0201s0113g0003g0110g0013Q10/k1000g0101s0211s0202",
    "g0111g0102s0212s0203k1001g0112g0200k1002g0103s0213g0113g0210",
    "Q11/g0201g0211A11/g0202g0212o1100g0203g0213Q12/o1101A12/o110",
    "2o1103o1200T11/s1100s1110o1201o1202s1101s1111o1203T12/s1102s",
    "1112s1200s1210s1201s1103g1100s1211s1113g1110g1101s1202g1111s",
    "1212g1102s1203g1112g1200s1213g1103g1210g1113H01/g1201g1211g1",
    "202g1212g1203H12/g1213H22/",
)
GROUPS = ((0, 5),)


def read_plan():
    text = "".join(PLAN)
    names = {"Q": "qkv", "A": "attn", "T": "tail", "H": "head", "k": "kv", "z": "wz", "x": "wx", "o": "ago", "s": "rs", "g": "agx"}
    plan, at, hooks, where = [], 0, None, 0
    while at < len(text):
        ch = text[at]
        at += 1
        if ch == "-":
            where += 1
        elif ch == "/":
            hooks = None
        elif ch.isupper():
            hooks, where = {}, -1
            plan.append((names[ch], int(text[at]), int(text[at + 1]), hooks))
            at += 2
        else:
            step = (names[ch],) + tuple(int(d) for d in text[at:at + 4])
            at += 4
            if hooks is None:
                plan.append(step)
            else:
                hooks.setdefault(where, []).append(step)
    return plan


def norm_rows(x, gain):
    x = x.astype(F32)
    inv = lax.rsqrt(jnp.mean(x * x, axis=-1, keepdims=True) + EPS)
    return (x * inv * gain).astype(BF)


def program(sizes, *refs):
    chunk, dim, hidden, vocab, scale = sizes
    half = chunk // 2
    unit = half // 4
    (xp, xr, tgt, again, mgain, fgain, cos, sin, wq, wk, wv, w_out, wg, wu, wd, wvoc) = refs[:16]
    (kvb, kvr, qb, og, og_last, pt, x1b, rr, rl, sr, sl, xg, wf, st_m, st_l, st_p) = refs[16:32]
    (va, vb, vc, vd, xs, lsem, ago_s, ago_r, agx_s, agx_r, rs_s, rs_r, kv_s, kv_r, wz_s, wz_r, wx_s, wx_r) = refs[32:]
    n_piece = 8
    piece = w_out.shape[1] // n_piece
    local = w_out.shape[1]

    z = lax.axis_index('model')
    r = lax.axis_index('resp')
    px = lax.axis_index('prompts')
    y, core = lax.div(r, 2), lax.rem(r, 2)
    r_core, r_y, r_yc = y * 2 + (1 - core), (1 - y) * 2 + core, (1 - y) * 2 + (1 - core)
    others = (r, r_core, r_y, r_yc)
    nx = 1 - px
    ending = []
    free = None

    def remote(src, dst, sems, at, dev):
        return pltpu.make_async_remote_copy(
            src, dst, sems[0].at[at], sems[1].at[at], device_id=dev, device_id_type=MESH)

    def when(cond, body):
        if cond is free:
            body()
        else:
            pl.when(cond)(body)

    def send(cond, *args):
        copy = lambda: remote(*args)
        when(cond, (lambda: copy().wait_send()) if ending else (lambda: copy().start()))

    def recv(cond, ref, *args):
        if not ending:
            when(cond, lambda: remote(ref, ref, *args).wait_recv())

    right, left = {'model': z + 1}, {'model': z - 1}
    to_y, to_core, to_x = {'resp': r_y}, {'resp': r_core}, {'prompts': nx}


    def gather(k, block, sems, at, own=None):
        sides = ((z - k, 0, right), (3 - z - k, 1, left))
        for room, side, to in sides:
            j = lax.rem(z + 4 + (2 * side - 1) * k, 4)
            src = own if own is not None and k == 0 else block(j)
            if k:
                recv(room >= 0, src, sems, at + (k - 1, side), to)
            if k < 3:
                ahead = z <= 2 if side == 0 else z >= 1
                send((room >= 0) & ahead, src, block(j), sems, at + (k, side), to)

    def heads_out(l, c, g, j):
        return (og_last if g else og).at[l, c, j]

    def step_ago(l, c, g, k):
        gather(k, lambda j: heads_out(l, c, g, j), (ago_s, ago_r), (l, c, g))

    def rows_at(g, j):
        return pl.ds(pl.multiple_of(g * half + j * unit, 16), unit)

    def step_agx(l, c, g, k):
        gather(k, lambda j: xg.at[l, c, rows_at(g, j)], (agx_s, agx_r), (l, c, g))

    def load(*pairs):
        copies = [pltpu.make_async_copy(s, d, lsem.at[i]) for i, (s, d) in enumerate(pairs)]
        for cp in copies:
            cp.start()
        for cp in copies:
            cp.wait()

    def add_rows(dst, *srcs):
        def body(i, carry):
            sl_ = pl.ds(pl.multiple_of(i * 16, 16), 16)
            total = srcs[0][sl_, :]
            for s in srcs[1:]:
                total = total + s[sl_, :]
            dst[sl_, :] = total
            return carry

        lax.fori_loop(0, unit // 16, body, 0)

    def step_rs(l, c, g, k):
        part, r_in, l_in, r_out, l_out = (lambda j: pt.at[l, c, rows_at(g, j)]), rr.at[l, c, g], rl.at[l, c, g], sr.at[l, c, g], sl.at[l, c, g]
        sems, at = (rs_s, rs_r), (l, c, g)
        if k < 3:
            send(z == 0, part(3 - k), r_in.at[k], sems, at + (k, 0), right)
            send(z == 3, part(k), l_in.at[k], sems, at + (k, 1), left)
        if k == 1:
            for cond, side, far, src, out, to in ((z == 1, 0, 3, r_in, r_out, right), (z == 2, 1, 0, l_in, l_out, left)):
                recv(cond, src.at[0], sems, at + (0, side), to)
                if not ending:
                    @pl.when(cond)
                    def _():
                        load((part(far), va), (src.at[0], vb))
                        add_rows(va, va, vb)
                        load((va, out.at[0]))
                send(cond, out.at[0], src.at[1], sems, at + (1, side), to)
        elif k == 2:
            mid = (z >= 1) & (z <= 2)
            sides = ((0, r_in, r_out, right), (1, l_in, l_out, left))
            for side, src, out, to in sides:
                recv(mid, src.at[1], sems, at + (1, side), to)
            if not ending:
                @pl.when(mid)
                def _():
                    load((part(z + 1), va), (r_in.at[1], vb), (part(z - 1), vc), (l_in.at[1], vd))
                    add_rows(va, va, vb)
                    add_rows(vc, vc, vd)
                    load((va, r_out.at[1]), (vc, l_out.at[1]))
            for side, src, out, to in sides:
                send(mid, out.at[1], src.at[2], sems, at + (2, side), to)
        elif k == 3 and not ending:
            ends = ((2, z >= 1, r_in.at[2], vb, right), (3, z <= 2, l_in.at[2], vc, left))
            for idx, cond, src, dst, to in ends:
                recv(cond, src, sems, at + (2, idx - 2), to)
            copies = [pltpu.make_async_copy(part(z), va, lsem.at[0]), pltpu.make_async_copy(x1b.at[l, c, g], xs, lsem.at[1])]
            for cp in copies:
                cp.start()
            for idx, cond, src, dst, _ in ends:
                @pl.when(cond)
                def _():
                    one = pltpu.make_async_copy(src, dst, lsem.at[idx])
                    one.start()
                    one.wait()

                @pl.when(jnp.logical_not(cond))
                def _():
                    dst[...] = jnp.zeros(dst.shape, F32)
            for cp in copies:
                cp.wait()

            def body(i, carry):
                s_ = pl.ds(pl.multiple_of(i * 16, 16), 16)
                total = va[s_, :] + (vb[s_, :] + vc[s_, :])
                xs[s_, :] = (xs[s_, :].astype(F32) + total).astype(BF)
                return carry

            lax.fori_loop(0, unit // 16, body, 0)
            load((xs, xg.at[l, c, rows_at(g, z)]))

    def step_kv(l, c, g, k):
        slots, sems = [kvr.at[l, i] for i in range(3)], (kv_s, kv_r)
        if k == 0:
            send(free, kvb.at[l, 0], slots[1], sems, (l, 1), to_y)
            send(free, kvb.at[l, 0], slots[0], sems, (l, 0), to_core)
        elif k == 1:
            recv(free, slots[1], sems, (l, 1), to_y)
            send(free, slots[1], slots[2], sems, (l, 2), to_core)
        else:
            recv(free, slots[0], sems, (l, 0), to_core)
            recv(free, slots[2], sems, (l, 2), to_core)

    def rows_of(j, rr_, xx):
        return pl.ds(pl.multiple_of(j * local + (xx * 4 + rr_) * piece, 16), piece)

    def step_wz(l, c, g, k):
        own = w_out.at[l, pl.ds(pl.multiple_of((px * 4 + r) * piece, 16), piece), :]
        gather(k, lambda j: wf.at[l, rows_of(j, r, px), :], (wz_s, wz_r), (l,), own)

    def step_wx(l, c, g, k):
        for s in range(3):
            j = lax.rem(z + 1 + s, 4)

            def push(i, place, to):
                at = wf.at[l, rows_of(j, *place), :]
                send(free, at, at, (wx_s, wx_r), (l, i, s), to)

            def pull(i, place, to):
                recv(free, wf.at[l, rows_of(j, *place), :], (wx_s, wx_r), (l, i, s), to)

            here, over_y, over_x, over_xy = (r, px), (r_y, px), (r, nx), (r_y, nx)
            if k == 0:
                push(0, here, to_y)
                push(1, here, to_x)
            elif k == 1:
                pull(0, over_y, to_y)
                push(2, over_y, to_x)
            elif k == 2:
                pull(1, over_x, to_x)
                pull(2, over_xy, to_x)
                for i, place in enumerate((here, over_y, over_x, over_xy)):
                    push(3 + i, place, to_core)
            else:
                for i, place in enumerate(((r_core, px), (r_yc, px), (r_core, nx), (r_yc, nx))):
                    pull(3 + i, place, to_core)

    steps = {"ago": step_ago, "agx": step_agx, "rs": step_rs, "kv": step_kv, "wz": step_wz, "wx": step_wx}

    def emit(item):
        steps[item[0]](*item[1:])

    def pre(hooks):
        for item in hooks.get(-1, []):
            emit(item)

    def loop(n, body, hooks, base):
        begin = 0
        for i in range(n):
            if hooks.get(base + i) or i == n - 1:
                lax.fori_loop(begin, i + 1, lambda k, carry: (body(k), carry)[1], 0)
                begin = i + 1
                for item in hooks.get(base + i, []):
                    emit(item)


    def load_x(l, c, x_vm, sem, first=0):
        rows = pl.ds(first, x_vm.shape[0])
        if l:
            src = xg.at[l - 1, c, rows]
        elif c:
            src = xr.at[0, pl.ds((c - 1) * chunk, chunk)]
        else:
            src = xp
        copy = pltpu.make_async_copy(src, x_vm, sem.at[0])
        copy.start()
        return copy

    def norm_all(src, dst, gain):
        rows = src.shape[0]

        def body(i, carry):
            s_ = pl.ds(pl.multiple_of(i * 32, 32), 32)
            dst[s_, :] = norm_rows(src[s_, :], gain)
            return carry

        lax.fori_loop(0, rows // 32, body, 0)

    def task_qkv(l, c, hooks):
        with_q = not (l == 1 and c == 0)
        kinds = (wk, wq, wv) if with_q else (wk, wv)
        n_w = NH * len(kinds)

        def scoped(x_vm, w_vm, o_vm, cs_vm, x_sems, w_sems, o_sems, c_sems):
            c_copies = [pltpu.make_async_copy(src.at[c], cs_vm.at[i], c_sems.at[i]) for i, src in enumerate((cos, sin))]
            w_copies = [pltpu.make_async_copy(w.at[l], w_vm.at[NH * i:NH * (i + 1)], w_sems.at[i]) for i, w in enumerate(kinds)]
            for cp in c_copies + w_copies:
                cp.start()
            pre(hooks)
            load_x(l, c, x_vm, x_sems).wait()
            norm_all(x_vm, x_vm, again[l:l + 1, :])
            for cp in c_copies + w_copies:
                cp.wait()
            cs, sn = cs_vm[0], cs_vm[1]

            def rope(part):
                return part * cs + pltpu.roll(part, HD // 2, 1) * sn

            def pair(i, ropes):
                both = jnp.concatenate([w_vm[i], w_vm[i + 1]], axis=1)
                full = jnp.dot(x_vm[...], both, preferred_element_type=F32)
                for n, with_rope in enumerate(ropes):
                    part = full[:, n * HD:(n + 1) * HD]
                    o_vm[i + n] = (rope(part) if with_rope else part).astype(BF)

            n_rope = n_w - NH

            loop(n_rope // 2, lambda i: pair(2 * i, (True, True)), hooks, 0)
            first = n_rope
            if n_rope % 2:
                pair(n_rope - 1, (True, False))
                first = n_rope + 1

            loop(2, lambda i: pair(first + 2 * i, (False, False)), hooks, 5)
            if first + 4 < n_w:
                o_vm[n_w - 1] = jnp.dot(x_vm[...], w_vm[n_w - 1], preferred_element_type=F32).astype(BF)
            outs = [(o_vm.at[0:NH], kvb.at[l, c, 0:NH]), (o_vm.at[n_w - NH:n_w], kvb.at[l, c, NH:2 * NH])]
            if with_q:
                outs.append((o_vm.at[NH:2 * NH], qb.at[l, c]))
            o_copies = [pltpu.make_async_copy(s, d, o_sems.at[i]) for i, (s, d) in enumerate(outs)]
            for cp in o_copies:
                cp.start()
            for cp in o_copies:
                cp.wait()

        pl.run_scoped(
            scoped, pltpu.VMEM((chunk, dim), BF), pltpu.VMEM((n_w, dim, HD), BF), pltpu.VMEM((n_w, chunk, HD), BF),
            pltpu.VMEM((2, chunk, HD), F32), DMA((1,)), DMA((3,)), DMA((3,)), DMA((2,)),
        )

    def task_attn(l, c, hooks):
        blocks = [kvb.at[l, 0], kvr.at[l, 0], kvr.at[l, 1], kvr.at[l, 2]] + [kvb.at[l, i] for i in range(1, c + 1)]
        n_blk = len(blocks)
        if c == 0:
            plan = [(0, "causal")] + [(m, "if") for m in (1, 2, 3)]
        else:
            plan = [(b, "causal" if b == n_blk - 1 else "full") for b in range(n_blk)]
        coef = scale * LOG2E

        def scoped(q_vm, kv_vm, s_vm, mx_vm, l_vm, acc_vm, o_vm, sems):
            copies = [pltpu.make_async_copy(qb.at[l, c], q_vm, sems.at[n_blk])]
            copies += [pltpu.make_async_copy(src, kv_vm.at[b], sems.at[b]) for b, src in enumerate(blocks)]
            pre(hooks)
            for cp in copies:
                cp.start()
            for cp in copies:
                cp.wait()

            def head_body(h):
                mx_vm[...] = jnp.full(mx_vm.shape, -jnp.inf, F32)
                l_vm[...] = jnp.zeros(l_vm.shape, F32)
                acc_vm[...] = jnp.zeros(acc_vm.shape, F32)

                def scores(b, causal):
                    s = lax.dot_general(q_vm[h], kv_vm[b, h], NT, preferred_element_type=F32)
                    if causal:
                        row = lax.broadcasted_iota(jnp.int32, s.shape, 0)
                        col = lax.broadcasted_iota(jnp.int32, s.shape, 1)
                        s = jnp.where(row >= col, s, -jnp.inf)
                    s_vm[:, b * chunk:(b + 1) * chunk] = s
                    top = mx_vm[...]
                    for t in range(chunk // HD):
                        top = jnp.maximum(top, s[:, t * HD:(t + 1) * HD])
                    mx_vm[...] = top

                def mix(b, m):
                    p = jnp.exp2((s_vm[:, b * chunk:(b + 1) * chunk] - m) * coef)
                    total = l_vm[...]
                    for t in range(chunk // HD):
                        total = total + p[:, t * HD:(t + 1) * HD]
                    l_vm[...] = total
                    acc_vm[...] += jnp.dot(p.astype(BF), kv_vm[b, NH + h], preferred_element_type=F32)

                for b, kind in plan:
                    if kind == "if":
                        pl.when(others[b] < r)(functools.partial(scores, b, False))
                    else:
                        scores(b, kind == "causal")
                m = jnp.max(mx_vm[...], axis=1, keepdims=True)
                for b, kind in plan:
                    if kind == "if":
                        pl.when(others[b] < r)(functools.partial(mix, b, m))
                    else:
                        mix(b, m)
                out = (acc_vm[...] / jnp.sum(l_vm[...], axis=1, keepdims=True)).astype(BF)
                o_vm[:, pl.ds(pl.multiple_of(h * HD, HD), HD)] = out

            for g, (first, end) in enumerate(GROUPS):
                lax.fori_loop(first, end, lambda h, carry: (head_body(h), carry)[1], 0)
                out_copy = pltpu.make_async_copy(o_vm.at[:, first * HD:end * HD], heads_out(l, c, g, z), sems.at[0])
                out_copy.start()
                out_copy.wait()
                for item in hooks.get(end - 1, []):
                    emit(item)

        pl.run_scoped(
            scoped, pltpu.VMEM((NH, chunk, HD), BF), pltpu.VMEM((n_blk, 2 * NH, chunk, HD), BF),
            pltpu.VMEM((chunk, n_blk * chunk), F32), pltpu.VMEM((chunk, HD), F32), pltpu.VMEM((chunk, HD), F32),
            pltpu.VMEM((chunk, HD), F32), pltpu.VMEM((chunk, NH * HD), BF), DMA((n_blk + 1,)),
        )

    def task_tail(l, c, hooks):
        full_blocks, rest = hidden // 256, hidden % 256

        def scoped(o_vm, x_vm, wo_vm, wg_vm, wu_vm, wd_vm, acc_vm, in_vm, o_sems, x_sems, wo_sems, w_sems, p_sems):
            wo_copies = [pltpu.make_async_copy(
                w_out.at[l], wo_vm.at[pl.ds(pl.multiple_of(z * local, 128), local), :], wo_sems.at[0])]
            for s in (1, 2, 3):
                rows = pl.ds(pl.multiple_of(lax.rem(z + s, 4) * local, 128), local)
                wo_copies.append(pltpu.make_async_copy(wf.at[l, rows, :], wo_vm.at[rows, :], wo_sems.at[s]))
            for cp in wo_copies:
                cp.start()
            x_copy = load_x(l, c, x_vm, x_sems)
            w_copies = [pltpu.make_async_copy(s.at[l], d, w_sems.at[i]) for i, (s, d) in enumerate(((wg, wg_vm), (wu, wu_vm), (wd, wd_vm)))]
            for cp in w_copies:
                cp.start()
            pre(hooks)
            o_copies = []
            for j in range(4):
                for g, (first, end) in enumerate(GROUPS):
                    cols = o_vm.at[:, j * local + first * HD:j * local + end * HD]
                    o_copies.append(pltpu.make_async_copy(heads_out(l, c, g, j), cols, o_sems.at[j, g]))
            for cp in o_copies:
                cp.start()
            for cp in wo_copies + o_copies:
                cp.wait()
            wide = dim // 5

            def out_body(i):
                cols = pl.ds(pl.multiple_of(i * wide, 128), wide)
                acc_vm[:, cols] = jnp.dot(o_vm[...], wo_vm[:, cols], preferred_element_type=F32)

            loop(5, out_body, hooks, 0)
            x_copy.wait()
            gain = mgain[l:l + 1, :]

            def finish(i, carry):
                s_ = pl.ds(pl.multiple_of(i * 32, 32), 32)
                x1 = (x_vm[s_, :].astype(F32) + acc_vm[s_, :]).astype(BF)
                x_vm[s_, :] = x1
                o_vm[s_, :] = norm_rows(x1, gain)
                return carry

            lax.fori_loop(0, chunk // 32, finish, 0)
            x1_copies = [
                pltpu.make_async_copy(
                    x_vm.at[pl.ds(pl.multiple_of(g * half + z * unit, 16), unit), :], x1b.at[l, c, g], x_sems.at[g])
                for g in range(2)
            ]
            for cp in x1_copies:
                cp.start()
            w_copies[0].wait()
            w_copies[1].wait()

            def gate_up(rows, cols):
                gate = lax.dot_general(o_vm[...], wg_vm[rows, :], NT, preferred_element_type=F32)
                up = lax.dot_general(o_vm[...], wu_vm[rows, :], NT, preferred_element_type=F32)
                in_vm[:, cols] = (jax.nn.silu(gate) * up).astype(BF)

            def gate_body(i):
                s_ = pl.ds(pl.multiple_of(i * 256, 256), 256)
                gate_up(s_, s_)

            loop(full_blocks, gate_body, hooks, 5)
            if rest:
                s_ = pl.ds(full_blocks * 256, rest)
                gate_up(s_, s_)
            w_copies[2].wait()

            for cp in x1_copies:
                cp.wait()
            for g in range(2):
                top = g * half

                def down_body(i):
                    cols = pl.ds(pl.multiple_of(i * wide, 128), wide)
                    acc_vm[top:top + half, cols] = jnp.dot(in_vm[top:top + half, :], wd_vm[:, cols], preferred_element_type=F32)

                lax.fori_loop(0, 5, lambda i, carry: (down_body(i), carry)[1], 0)
                p_copy = pltpu.make_async_copy(acc_vm.at[top:top + half], pt.at[l, c, pl.ds(top, half)], p_sems.at[g])
                p_copy.start()
                p_copy.wait()
                for item in hooks.get(9 + full_blocks + 5 * g, []):
                    emit(item)

        pl.run_scoped(
            scoped, pltpu.VMEM((chunk, dim), BF), pltpu.VMEM((chunk, dim), BF), pltpu.VMEM((4 * local, dim), BF),
            pltpu.VMEM((hidden, dim), BF), pltpu.VMEM((hidden, dim), BF), pltpu.VMEM((hidden, dim), BF),
            pltpu.VMEM((chunk, dim), F32), pltpu.VMEM((chunk, hidden), BF),
            DMA((4, 2)), DMA((2,)), DMA((4,)), DMA((3,)), DMA((2,)),
        )

    def task_head(mode, c, hooks):
        wide = 1024
        n_steps = vocab // (2 * wide)
        rows = half if mode else chunk
        begin = (mode - 1) * half if mode else 0
        out = c - 1

        def scoped(h_vm, w_vm, a_vm, b_vm, mx_vm, sum_vm, pick_vm, want_vm, x_sems, w_sems):
            def fetch(i, slot):
                cols = pl.ds(pl.multiple_of(i * 2 * wide, 2 * wide), 2 * wide)
                return pltpu.make_async_copy(wvoc.at[:, cols], w_vm.at[slot], w_sems.at[slot])

            fetch(0, 0).start()
            pre(hooks)
            load_x(2, c, h_vm, x_sems, begin).wait()
            norm_all(h_vm, h_vm, fgain[...])
            want_vm[...] = tgt[out, begin:begin + rows, :]
            b_vm[...] = jnp.full(b_vm.shape, NEG, F32)
            mx_vm[...] = jnp.full(mx_vm.shape, NEG, F32)
            sum_vm[...] = jnp.zeros(sum_vm.shape, F32)
            pick_vm[...] = jnp.zeros(pick_vm.shape, F32)

            def fold(src, first, at):
                old = mx_vm[at, :]
                tiles = [src[at, t * HD:(t + 1) * HD] for t in range(wide // HD)]
                top = old
                for tile in tiles:
                    top = jnp.maximum(top, tile)
                total = sum_vm[at, :] * jnp.exp(old - top)
                pick = pick_vm[at, :]
                lane = lax.broadcasted_iota(jnp.int32, old.shape, 1)
                off = want_vm[at, :] - first - lane
                for t, tile in enumerate(tiles):
                    total = total + jnp.exp(tile - top)
                    pick = pick + jnp.where(off == t * HD, tile, 0.0)
                mx_vm[at, :] = top
                sum_vm[at, :] = total
                pick_vm[at, :] = pick

            def folds(src, first, lo, n):
                step = lambda i, carry: (fold(src, first, pl.ds(pl.multiple_of(lo + i * 32, 32), 32)), carry)[1]
                lax.fori_loop(0, n // 32, step, 0)

            def phase(dst, slot, col, src, first):
                n_sub = wide // 256
                n = rows // n_sub
                for sub in range(n_sub):
                    lo = sub * 256
                    dst[:, lo:lo + 256] = jnp.dot(
                        h_vm[...], w_vm[slot, :, col + lo:col + lo + 256], preferred_element_type=F32)
                    folds(src, first, sub * n, n)

            def body(i):
                slot = lax.rem(i, 2)

                @pl.when(i + 1 < n_steps)
                def _():
                    fetch(i + 1, 1 - slot).start()

                fetch(i, slot).wait()
                base = i * 2 * wide
                phase(a_vm, slot, 0, b_vm, jnp.where(i == 0, vocab * 8, base - wide))
                phase(b_vm, slot, wide, a_vm, base)

            loop(n_steps, body, hooks, 0)
            folds(b_vm, vocab - wide, 0, rows)
            top = jnp.max(mx_vm[...], axis=1, keepdims=True)
            total = jnp.sum(sum_vm[...] * jnp.exp(mx_vm[...] - top), axis=1, keepdims=True)
            pick = jnp.sum(pick_vm[...], axis=1, keepdims=True)
            st_m[out, begin:begin + rows, :] = jnp.broadcast_to(top, (rows, HD))
            st_l[out, begin:begin + rows, :] = jnp.broadcast_to(total, (rows, HD))
            st_p[out, begin:begin + rows, :] = jnp.broadcast_to(pick, (rows, HD))

        pl.run_scoped(
            scoped, pltpu.VMEM((rows, dim), BF), pltpu.VMEM((2, dim, 2 * wide), BF),
            pltpu.VMEM((rows, wide), F32), pltpu.VMEM((rows, wide), F32), pltpu.VMEM((rows, HD), F32),
            pltpu.VMEM((rows, HD), F32), pltpu.VMEM((rows, HD), F32), pltpu.VMEM((rows, 1), jnp.int32), DMA((1,)), DMA((2,)),
        )

    tasks = {"qkv": task_qkv, "attn": task_attn, "tail": task_tail, "head": task_head}

    barrier = pltpu.get_barrier_semaphore()

    def greet(dev):
        pl.semaphore_signal(barrier, inc=1, device_id=dev, device_id_type=MESH)

    for dev in (to_core, to_y, to_x):
        greet(dev)
    pl.when(z <= 2)(lambda: greet(right))
    pl.when(z >= 1)(lambda: greet(left))
    pl.semaphore_wait(barrier, 3 + lax.div(z + 2, 3) + lax.div(5 - z, 3))

    plan = read_plan()
    for entry in plan:
        if entry[0] in tasks:
            tasks[entry[0]](*entry[1:])
        else:
            emit(entry)
    ending.append(True)
    for entry in plan:
        for item in (sum(entry[-1].values(), []) if entry[0] in tasks else [entry]):
            emit(item)


def solution(mesh):
    row_axes = ('prompts', 'resp')
    rows, whole, second, third = P(row_axes), P(), P(None, 'model'), P(None, None, 'model')
    in_specs = (rows, rows, rows, rows, whole, third, third, third, second, whole, third, third, second, whole, second)
    groups = mesh.shape['resp']

    def device_step(x_prompt, x_resp, targets, resp_lens, attn_gain, w_query, w_key, w_value, w_out, mlp_gain, w_gate, w_up, w_down, final_gain, w_vocab):
        chunk, dim = x_prompt.shape
        resp_len = x_resp.shape[1]
        prompt_len = chunk * groups
        n_l = w_query.shape[0]
        hidden = w_gate.shape[2]
        vocab = w_vocab.shape[1]
        local = w_out.shape[1] * HD
        z = lax.axis_index('model')
        r = lax.axis_index('resp')
        heads_first = lambda w: jnp.transpose(w, (0, 2, 1, 3))

        tok_pos = jnp.concatenate([r * chunk + jnp.arange(chunk), prompt_len + jnp.arange(resp_len)])
        half = HD // 2
        frequency = ROPE_BASE ** (-jnp.arange(half, dtype=F32) / half)
        angles = tok_pos.astype(F32)[:, None] * frequency
        cos, sin = jnp.cos(angles), jnp.sin(angles)
        n_resp = resp_len // chunk
        n_c = 1 + n_resp
        cos = jnp.concatenate([cos, cos], axis=1).reshape(n_c, chunk, HD)
        sin = jnp.concatenate([-sin, sin], axis=1).reshape(n_c, chunk, HD)
        tgt = (targets[0] - z * vocab).reshape(n_resp, chunk, 1)
        unit = chunk // 8

        sds = jax.ShapeDtypeStruct
        out_shape = [
            sds((n_l, n_c, 2 * NH, chunk, HD), BF), sds((n_l, 3, 2 * NH, chunk, HD), BF), sds((n_l, n_c, NH, chunk, HD), BF),
            sds((n_l, n_c, 4, chunk, 5 * HD), BF), sds((n_l, n_c, 4, chunk, HD), BF), sds((n_l, n_c, chunk, dim), F32), sds((n_l, n_c, 2, unit, dim), BF),
            sds((n_l, n_c, 2, 3, unit, dim), F32), sds((n_l, n_c, 2, 3, unit, dim), F32),
            sds((n_l, n_c, 2, 2, unit, dim), F32), sds((n_l, n_c, 2, 2, unit, dim), F32),
            sds((n_l, n_c, chunk, dim), BF), sds((n_l, 4 * local, dim), BF),
        ] + [sds((n_resp, chunk, HD), F32)] * 3
        gsem = lambda g: DMA((n_l, n_c) + g + (3, 2))
        outs = pl.pallas_call(
            functools.partial(program, (chunk, dim, hidden, vocab, HD ** -0.5)),
            out_shape=out_shape,
            in_specs=[ANY, ANY, VMEM, VMEM, VMEM, VMEM] + [ANY] * 10,
            out_specs=[ANY] * 13 + [VMEM] * 3,
            scratch_shapes=[pltpu.VMEM((unit, dim), F32)] * 4 + [pltpu.VMEM((unit, dim), BF), DMA((4,))] + [gsem((1,))] * 2 + [gsem((2,))] * 4
            + [DMA((n_l, 3))] * 2 + [DMA((n_l, 3, 2))] * 2 + [DMA((n_l, 7, 3))] * 2,
            compiler_params=pltpu.CompilerParams(collective_id=0, has_side_effects=True, vmem_limit_bytes=67043328),
            name="decoder",
        )(x_prompt, x_resp, tgt, attn_gain, mlp_gain, final_gain[None], cos, sin, heads_first(w_query), heads_first(w_key), heads_first(w_value), w_out.reshape(n_l, local, dim), jnp.transpose(w_gate, (0, 2, 1)), jnp.transpose(w_up, (0, 2, 1)), w_down, w_vocab)
        stats = jnp.stack([s[:, :, 0].reshape(resp_len) for s in outs[13:]])
        stats = lax.all_gather(stats, 'model', axis=0)
        row_max = jnp.max(stats[:, 0], axis=0)
        exp_total = jnp.sum(stats[:, 1] * jnp.exp(stats[:, 0] - row_max), axis=0)
        picked = jnp.sum(stats[:, 2], axis=0)
        log_probs = picked - row_max - jnp.log(exp_total)
        log_probs = jnp.where(jnp.arange(resp_len) < resp_lens[0], log_probs, 0.0)
        return log_probs[None, :]

    return jax.shard_map(device_step, mesh=mesh, in_specs=in_specs, out_specs=rows, check_vma=False)
```

time: 2400 us -> 1130 us (0.47)
  waiting for transfers between devices: 1760 us -> 0 us
  Pallas kernels: 0 us -> 1100 us
  matrix products: 421 us -> 0 us
  other arithmetic: 144 us -> 5.9 us
  local copies, waits for them, and re-layouts: 37.7 us -> 6.23 us
    psum x4 -> x0, waiting for transfers between devices: 1750 us -> none  [the longest x2 880 us: device_step(): lax.psum(attn_part, 'model')]
    pallas_call x0 -> x1, Pallas kernels: none -> 1100 us  [device_step(): pl.pallas_call(functools.partial(program, (chunk, dim, hidden, vocab, HD...]
    dot_general x14 -> x0, matrix products: 393 us -> none  [the longest x1 100 us: device_step(): jnp.dot(rms_norm(residual, final_gain), w_vocab, preferred_element_type=j...]
    reduce_sum x8 -> x2, other arithmetic: 112 us -> 0.08 us  [the longest x1 0.06 us: device_step(): picked = jnp.sum(stats[:, 2], axis=0)]
    unnamed x4 -> x0, matrix products: 27.9 us -> none
  transfers between devices with their start and end apart: 8 -> 0, of which waited for: 5 -> 0; matrix products, arithmetic and copies ran while one was open for 7% -> 0% of each run, Pallas kernels for 0% -> 0%
where the time goes in v1:
time: 1130 us
  Pallas kernels  1100 us (97%)
  blocking collectives  13.1 us (1%)
    pallas_call x1, Pallas kernels, device_step(): pl.pallas_call(functools.partial(program, (chunk, dim, hidden, vocab, HD...  1100 us

profile of v1, /device:TPU:0, one launch (start us, length us, event | category | flops | bytes accessed | tf_op | source)
XLA Modules:
  0.0 1129.2 jit_solution(3474091854450453356)
XLA Ops:
  0.1 2.8 fusion
  2.9 1.6 pad_maximum_fusion
  4.5 0.7 subtract_reduce_fusion
  5.2 1.1 sub.56.refs_2_
  6.4 1.3 broadcast_in_dim.6.refs_5_
  7.7 1102.8 %decoder.1 = (bf16[2,3,10,512,128]{4,3,2,1,0:T(8,128)(2,1)}, bf16[2,3,10,512,128]{4,3,2,1,0:T(8,128)(2,1)}, bf16[2,3,5,512,128]{4,3,2,1,0:T(8,128)(2,1)}, bf16[2...) custom-call(bf16[512,2560]{1,0:T(8,128)(2,1)} %refs_0_.1, ...), custom_call_target="tpu_custom_call" | custom-call | tf_op jit(solution)/shard_map/decoder/pallas_call | solution.py:659
  1110.5 1.3 slice_reduce_fusion.2
  1111.7 1.3 slice_reduce_fusion.1
  1113.0 1.3 slice_reduce_fusion
  1114.3 13.1 %all-gather.1 = f32[4,3,1024]{2,1,0:T(4,128)S(1)} all-gather(f32[1,3,1024]{2,1,0:T(4,128)S(1)} %maximum_bitcast_fusion), channel_id=2, replica_groups=mesh['prompts'=2,'model'=4,'resp'=4] {'model'}, dimensions={0}, use_global_device_ids=true | all-gather | bytes 61440 | tf_op jit(solution)/shard_map/all_gather | solution.py:670
  1127.4 0.1 slice_reduce_fusion.3
  1128.2 0.6 compare_select_fusion
  (11 shorter events, 0.1 us)

commit v2 on v1

--- a/solution.py
+++ b/solution.py
@@ -22,40 +22,37 @@
 
 
 PLAN = (
-    "z0000Q00/k0000z0001Q02/z0002Q01/k0001z0003x0000k0002A00/o000",
-    "0A01/x0001o0001o0100A02/x0002o0002z1000o0101o0200x0003o0003T",
-    "00/s0000z1001s0010o0102o0201z1002s0001s0011o0103T01/s0002s00",
-    "12z1003x1000s0100o0202s0110s0101x1001s0003g0000s0013g0010s01",
-    "11o0203T02/g0001g0011x1002s0102s0112s0200g0002x1003s0210g001",
-    "2s0103g0100s0201s0113g0003g0110g0013Q10/k1000g0101s0211s0202",
-    "g0111g0102s0212s0203k1001g0112g0200k1002g0103s0213g0113g0210",
-    "Q11/g0201g0211A11/g0202g0212o1100g0203g0213Q12/o1101A12/o110",
-    "2o1103o1200T11/s1100s1110o1201o1202s1101s1111o1203T12/s1102s",
-    "1112s1200s1210s1201s1103g1100s1211s1113g1110g1101s1202g1111s",
-    "1212g1102s1203g1112g1200s1213g1103g1210g1113H01/g1201g1211g1",
-    "202g1212g1203H12/g1213H22/",
+    "z00Q00-------z01/k00Q01-------z02/Q02-------z03x00/k01A00k02",
+    "-----o00/A01-----o01o10x01/A02-----o02o20/x02o11x03o03T00---",
+    "--o21---z30--------s00o12-----s04/o22s01z31s05o13T01-----s02",
+    "o23---s06z32--------s10-----s03/T02-----s07g00g04s11z33x30--",
+    "----s14-----g01-----g05s12x31/s15g02g06s20s13x32Q10g10g03s24",
+    "g07-------x33/k30s16g11s21s17k31g12g14s25k32s22g13g15s26s23g",
+    "20g16s27g24g21Q11g17-------g25/g22A11-----g23g26o40/Q12g27/o",
+    "41A12-----o42o50/T11o43--------o51--------s40-----s44o52/T12",
+    "o53--------s41---s45-----s50/s42s46s43g40s47g44s51g41s54g45s",
+    "52g42g46s55s53g50g43H01g47----g51s56----g52s57g54/H12g53----",
+    "g55----g56/H22g57/",
 )
 GROUPS = ((0, 5),)
 
 
 def read_plan():
     text = "".join(PLAN)
-    names = {"Q": "qkv", "A": "attn", "T": "tail", "H": "head", "k": "kv", "z": "wz", "x": "wx", "o": "ago", "s": "rs", "g": "agx"}
-    plan, at, hooks, where = [], 0, None, 0
-    while at < len(text):
-        ch = text[at]
-        at += 1
-        if ch == "-":
+    names = {"Q": "qkv", "A": "attn", "T": "tail", "H": "head"}
+    plan, hooks, where = [], None, 0
+    marks = iter(text)
+    for mark in marks:
+        if mark == "-":
             where += 1
-        elif ch == "/":
+        elif mark == "/":
             hooks = None
-        elif ch.isupper():
+        elif mark.isupper():
             hooks, where = {}, -1
-            plan.append((names[ch], int(text[at]), int(text[at + 1]), hooks))
-            at += 2
+            plan.append((names[mark], int(next(marks)), int(next(marks)), hooks))
         else:
-            step = (names[ch],) + tuple(int(d) for d in text[at:at + 4])
-            at += 4
+            at, k = int(next(marks)), int(next(marks))
+            step = (mark, at // 3, at % 3, k // 4, k % 4)
             if hooks is None:
                 plan.append(step)
             else:
@@ -108,8 +105,8 @@
         if not ending:
             when(cond, lambda: remote(ref, ref, *args).wait_recv())
 
-    right, left = {'model': z + 1}, {'model': z - 1}
-    to_y, to_core, to_x = {'resp': r_y}, {'resp': r_core}, {'prompts': nx}
+    right, left = (px, z + 1, r), (px, z - 1, r)
+    to_y, to_core, to_x = (px, z, r_y), (px, z, r_core), (nx, z, r)
 
 
     def gather(k, block, sems, at, own=None):
@@ -258,7 +255,7 @@
                 for i, place in enumerate(((r_core, px), (r_yc, px), (r_core, nx), (r_yc, nx))):
                     pull(3 + i, place, to_core)
 
-    steps = {"ago": step_ago, "agx": step_agx, "rs": step_rs, "kv": step_kv, "wz": step_wz, "wx": step_wx}
+    steps = {"o": step_ago, "g": step_agx, "s": step_rs, "k": step_kv, "z": step_wz, "x": step_wx}
 
     def emit(item):
         steps[item[0]](*item[1:])
@@ -275,6 +272,12 @@
                 begin = i + 1
                 for item in hooks.get(base + i, []):
                     emit(item)
+
+    def steps_of(n, body, hooks, base):
+        for i in range(n):
+            body(i)
+            for item in hooks.get(base + i, []):
+                emit(item)
 
 
     def load_x(l, c, x_vm, sem, first=0):
@@ -328,13 +331,13 @@
 
             n_rope = n_w - NH
 
-            loop(n_rope // 2, lambda i: pair(2 * i, (True, True)), hooks, 0)
+            steps_of(n_rope // 2, lambda i: pair(2 * i, (True, True)), hooks, 0)
             first = n_rope
             if n_rope % 2:
                 pair(n_rope - 1, (True, False))
                 first = n_rope + 1
 
-            loop(2, lambda i: pair(first + 2 * i, (False, False)), hooks, 5)
+            steps_of(2, lambda i: pair(first + 2 * i, (False, False)), hooks, 5)
             if first + 4 < n_w:
                 o_vm[n_w - 1] = jnp.dot(x_vm[...], w_vm[n_w - 1], preferred_element_type=F32).astype(BF)
             outs = [(o_vm.at[0:NH], kvb.at[l, c, 0:NH]), (o_vm.at[n_w - NH:n_w], kvb.at[l, c, NH:2 * NH])]
@@ -450,10 +453,10 @@
             wide = dim // 5
 
             def out_body(i):
-                cols = pl.ds(pl.multiple_of(i * wide, 128), wide)
+                cols = pl.ds(i * wide, wide)
                 acc_vm[:, cols] = jnp.dot(o_vm[...], wo_vm[:, cols], preferred_element_type=F32)
 
-            loop(5, out_body, hooks, 0)
+            steps_of(5, out_body, hooks, 0)
             x_copy.wait()
             gain = mgain[l:l + 1, :]
 
@@ -481,10 +484,10 @@
                 in_vm[:, cols] = (jax.nn.silu(gate) * up).astype(BF)
 
             def gate_body(i):
-                s_ = pl.ds(pl.multiple_of(i * 256, 256), 256)
+                s_ = pl.ds(i * 256, 256)
                 gate_up(s_, s_)
 
-            loop(full_blocks, gate_body, hooks, 5)
+            steps_of(full_blocks, gate_body, hooks, 5)
             if rest:
                 s_ = pl.ds(full_blocks * 256, rest)
                 gate_up(s_, s_)
@@ -496,10 +499,10 @@
                 top = g * half
 
                 def down_body(i):
-                    cols = pl.ds(pl.multiple_of(i * wide, 128), wide)
+                    cols = pl.ds(i * wide, wide)
                     acc_vm[top:top + half, cols] = jnp.dot(in_vm[top:top + half, :], wd_vm[:, cols], preferred_element_type=F32)
 
-                lax.fori_loop(0, 5, lambda i, carry: (down_body(i), carry)[1], 0)
+                steps_of(5, down_body, {}, 0)
                 p_copy = pltpu.make_async_copy(acc_vm.at[top:top + half], pt.at[l, c, pl.ds(top, half)], p_sems.at[g])
                 p_copy.start()
                 p_copy.wait()
@@ -535,26 +538,24 @@
             sum_vm[...] = jnp.zeros(sum_vm.shape, F32)
             pick_vm[...] = jnp.zeros(pick_vm.shape, F32)
 
+            def narrow(x, op):
+                while x.shape[1] > HD:
+                    mid = x.shape[1] // 2
+                    x = op(x[:, :mid], x[:, mid:])
+                return x
+
             def fold(src, first, at):
-                old = mx_vm[at, :]
-                tiles = [src[at, t * HD:(t + 1) * HD] for t in range(wide // HD)]
-                top = old
-                for tile in tiles:
-                    top = jnp.maximum(top, tile)
-                total = sum_vm[at, :] * jnp.exp(old - top)
-                pick = pick_vm[at, :]
-                lane = lax.broadcasted_iota(jnp.int32, old.shape, 1)
-                off = want_vm[at, :] - first - lane
-                for t, tile in enumerate(tiles):
-                    total = total + jnp.exp(tile - top)
-                    pick = pick + jnp.where(off == t * HD, tile, 0.0)
+                block, old = src[at, :], mx_vm[at, :]
+                top = jnp.maximum(old, narrow(block, jnp.maximum))
+                terms = jnp.exp(block - jnp.concatenate([top] * (wide // HD), axis=1))
+                hit = want_vm[at, :] - first == lax.broadcasted_iota(jnp.int32, block.shape, 1)
                 mx_vm[at, :] = top
-                sum_vm[at, :] = total
-                pick_vm[at, :] = pick
+                sum_vm[at, :] = sum_vm[at, :] * jnp.exp(old - top) + narrow(terms, jnp.add)
+                pick_vm[at, :] += narrow(jnp.where(hit, block, 0.0), jnp.add)
 
             def folds(src, first, lo, n):
-                step = lambda i, carry: (fold(src, first, pl.ds(pl.multiple_of(lo + i * 32, 32), 32)), carry)[1]
-                lax.fori_loop(0, n // 32, step, 0)
+                for i in range(n // 32):
+                    fold(src, first, pl.ds(lo + i * 32, 32))
 
             def phase(dst, slot, col, src, first):
                 n_sub = wide // 256
@@ -578,7 +579,8 @@
                 phase(b_vm, slot, wide, a_vm, base)
 
             loop(n_steps, body, hooks, 0)
-            folds(b_vm, vocab - wide, 0, rows)
+            last_fold = lambda i, carry: (fold(b_vm, vocab - wide, pl.ds(pl.multiple_of(i * 32, 32), 32)), carry)[1]
+            lax.fori_loop(0, rows // 32, last_fold, 0)
             top = jnp.max(mx_vm[...], axis=1, keepdims=True)
             total = jnp.sum(sum_vm[...] * jnp.exp(mx_vm[...] - top), axis=1, keepdims=True)
             pick = jnp.sum(pick_vm[...], axis=1, keepdims=True)

time: 1130 us -> 912 us (0.81)
  the two profiles are of different devices: /device:TPU:0 before, /device:TPU:7 now
where the time goes in v2:
time: 912 us; the launch traced here: 907 us
  Pallas kernels  884 us (97%)
  blocking collectives  10.2 us (1%)
    pallas_call x1, Pallas kernels, device_step(): pl.pallas_call(functools.partial(program, (chunk, dim, hidden, vocab, HD...  884 us

profile of v2, /device:TPU:7, one launch (start us, length us, event | category | flops | bytes accessed | tf_op | source)
XLA Modules:
  0.0 907.1 jit_solution(10555713366725284454)
XLA Ops:
  0.1 2.8 fusion
  2.9 1.6 pad_maximum_fusion
  4.5 0.7 subtract_reduce_fusion
  5.2 1.1 sub.56.refs_2_
  6.4 1.3 broadcast_in_dim.6.refs_5_
  7.7 883.7 %decoder.1 = (bf16[2,3,10,512,128]{4,3,2,1,0:T(8,128)(2,1)}, bf16[2,3,10,512,128]{4,3,2,1,0:T(8,128)(2,1)}, bf16[2,3,5,512,128]{4,3,2,1,0:T(8,128)(2,1)}, bf16[2...) custom-call(bf16[512,2560]{1,0:T(8,128)(2,1)} %refs_0_.1, ...), custom_call_target="tpu_custom_call" | custom-call | tf_op jit(solution)/shard_map/decoder/pallas_call | solution.py:661
  891.4 1.3 slice_reduce_fusion.2
  892.7 1.3 slice_reduce_fusion.1
  893.9 1.3 slice_reduce_fusion
  895.2 10.2 %all-gather.1 = f32[4,3,1024]{2,1,0:T(4,128)S(1)} all-gather(f32[1,3,1024]{2,1,0:T(4,128)S(1)} %maximum_bitcast_fusion), channel_id=2, replica_groups=mesh['prompts'=2,'model'=4,'resp'=4] {'model'}, dimensions={0}, use_global_device_ids=true | all-gather | bytes 61440 | tf_op jit(solution)/shard_map/all_gather | solution.py:672
  905.5 0.1 slice_reduce_fusion.3
  906.2 0.6 compare_select_fusion
  (11 shorter events, 0.1 us)

commit v3 on v2

--- a/solution.py
+++ b/solution.py
@@ -23,18 +23,20 @@
 
 PLAN = (
     "z00Q00-------z01/k00Q01-------z02/Q02-------z03x00/k01A00k02",
-    "-----o00/A01-----o01o10x01/A02-----o02o20/x02o11x03o03T00---",
-    "--o21---z30--------s00o12-----s04/o22s01z31s05o13T01-----s02",
-    "o23---s06z32--------s10-----s03/T02-----s07g00g04s11z33x30--",
-    "----s14-----g01-----g05s12x31/s15g02g06s20s13x32Q10g10g03s24",
-    "g07-------x33/k30s16g11s21s17k31g12g14s25k32s22g13g15s26s23g",
-    "20g16s27g24g21Q11g17-------g25/g22A11-----g23g26o40/Q12g27/o",
-    "41A12-----o42o50/T11o43--------o51--------s40-----s44o52/T12",
-    "o53--------s41---s45-----s50/s42s46s43g40s47g44s51g41s54g45s",
-    "52g42g46s55s53g50g43H01g47----g51s56----g52s57g54/H12g53----",
-    "g55----g56/H22g57/",
+    "---o00--o04/z30A01---o01x01--o05o10/A02---o02--o06x02o11/o03",
+    "o14o07o20x03T00-----o12o15---o21---o13-----o16s00-----o22s04",
+    "/T01z31o17-----o23s01---z32---s05-----z33x30-----s02/s06x31s",
+    "03g00o24s10s07g01g04o25x32s14g02x33g05o26T02s11g03g06s15o27-",
+    "----g07s12-----------s16s13-----g10/Q10-------s17g14g11s20/k",
+    "30s24g15g12s21g16Q11g13g17-------k31s25/A11k32---o40s22/o44o",
+    "41s26s23o45o42s27o46T11g20g24o43o47-----g21------g22-----g23",
+    "g25s40-----s44/g26Q12g27/s41A12---o50--o54s42/o51o55s45s43o5",
+    "2o56T12g40o53o57-----s46---g41--------s47g42g44s50-----g43/s",
+    "54g45g46H01s51g47----s52----s53g50s55/g51s56g52H12s57g54g53-",
+    "---g55----g56/g57H22/",
 )
-GROUPS = ((0, 5),)
+RADIX = {-5: (2, 3, 2, 3, 2), -3: (2, 7, 3), -2: (2, 3)}
+GROUPS = ((0, 3), (3, 5))
 
 
 def read_plan():
@@ -60,6 +62,14 @@
     return plan
 
 
+class Rows:
+    def __init__(self, buf, first):
+        self.buf, self.first, self.at = buf, first, self
+
+    def __getitem__(self, i):
+        return self.buf.at[self.first + i]
+
+
 def norm_rows(x, gain):
     x = x.astype(F32)
     inv = lax.rsqrt(jnp.mean(x * x, axis=-1, keepdims=True) + EPS)
@@ -88,8 +98,11 @@
     free = None
 
     def remote(src, dst, sems, at, dev):
+        slot = 0
+        for digit, base in zip(at, RADIX[-len(at)]):
+            slot = slot * base + digit
         return pltpu.make_async_remote_copy(
-            src, dst, sems[0].at[at], sems[1].at[at], device_id=dev, device_id_type=MESH)
+            src, dst, sems[0].at[slot], sems[1].at[slot], device_id=dev, device_id_type=MESH)
 
     def when(cond, body):
         if cond is free:
@@ -121,7 +134,7 @@
                 send((room >= 0) & ahead, src, block(j), sems, at + (k, side), to)
 
     def heads_out(l, c, g, j):
-        return (og_last if g else og).at[l, c, j]
+        return (og_last if g else og).at[l * 3 + c, j]
 
     def step_ago(l, c, g, k):
         gather(k, lambda j: heads_out(l, c, g, j), (ago_s, ago_r), (l, c, g))
@@ -130,7 +143,7 @@
         return pl.ds(pl.multiple_of(g * half + j * unit, 16), unit)
 
     def step_agx(l, c, g, k):
-        gather(k, lambda j: xg.at[l, c, rows_at(g, j)], (agx_s, agx_r), (l, c, g))
+        gather(k, lambda j: xg.at[l * 3 + c, rows_at(g, j)], (agx_s, agx_r), (l, c, g))
 
     def load(*pairs):
         copies = [pltpu.make_async_copy(s, d, lsem.at[i]) for i, (s, d) in enumerate(pairs)]
@@ -151,7 +164,7 @@
         lax.fori_loop(0, unit // 16, body, 0)
 
     def step_rs(l, c, g, k):
-        part, r_in, l_in, r_out, l_out = (lambda j: pt.at[l, c, rows_at(g, j)]), rr.at[l, c, g], rl.at[l, c, g], sr.at[l, c, g], sl.at[l, c, g]
+        part, r_in, l_in, r_out, l_out = (lambda j: pt.at[l * 3 + c, rows_at(g, j)]), *(Rows(buf, ((l * 3 + c) * 2 + g) * 3) for buf in (rr, rl, sr, sl))
         sems, at = (rs_s, rs_r), (l, c, g)
         if k < 3:
             send(z == 0, part(3 - k), r_in.at[k], sems, at + (k, 0), right)
@@ -184,7 +197,7 @@
             ends = ((2, z >= 1, r_in.at[2], vb, right), (3, z <= 2, l_in.at[2], vc, left))
             for idx, cond, src, dst, to in ends:
                 recv(cond, src, sems, at + (2, idx - 2), to)
-            copies = [pltpu.make_async_copy(part(z), va, lsem.at[0]), pltpu.make_async_copy(x1b.at[l, c, g], xs, lsem.at[1])]
+            copies = [pltpu.make_async_copy(part(z), va, lsem.at[0]), pltpu.make_async_copy(x1b.at[(l * 3 + c) * 2 + g], xs, lsem.at[1])]
             for cp in copies:
                 cp.start()
             for idx, cond, src, dst, _ in ends:
@@ -207,7 +220,7 @@
                 return carry
 
             lax.fori_loop(0, unit // 16, body, 0)
-            load((xs, xg.at[l, c, rows_at(g, z)]))
+            load((xs, xg.at[l * 3 + c, rows_at(g, z)]))
 
     def step_kv(l, c, g, k):
         slots, sems = [kvr.at[l, i] for i in range(3)], (kv_s, kv_r)
@@ -283,7 +296,7 @@
     def load_x(l, c, x_vm, sem, first=0):
         rows = pl.ds(first, x_vm.shape[0])
         if l:
-            src = xg.at[l - 1, c, rows]
+            src = xg.at[(l - 1) * 3 + c, rows]
         elif c:
             src = xr.at[0, pl.ds((c - 1) * chunk, chunk)]
         else:
@@ -470,7 +483,7 @@
             lax.fori_loop(0, chunk // 32, finish, 0)
             x1_copies = [
                 pltpu.make_async_copy(
-                    x_vm.at[pl.ds(pl.multiple_of(g * half + z * unit, 16), unit), :], x1b.at[l, c, g], x_sems.at[g])
+                    x_vm.at[pl.ds(pl.multiple_of(g * half + z * unit, 16), unit), :], x1b.at[(l * 3 + c) * 2 + g], x_sems.at[g])
                 for g in range(2)
             ]
             for cp in x1_copies:
@@ -503,7 +516,7 @@
                     acc_vm[top:top + half, cols] = jnp.dot(in_vm[top:top + half, :], wd_vm[:, cols], preferred_element_type=F32)
 
                 steps_of(5, down_body, {}, 0)
-                p_copy = pltpu.make_async_copy(acc_vm.at[top:top + half], pt.at[l, c, pl.ds(top, half)], p_sems.at[g])
+                p_copy = pltpu.make_async_copy(acc_vm.at[top:top + half], pt.at[l * 3 + c, pl.ds(top, half)], p_sems.at[g])
                 p_copy.start()
                 p_copy.wait()
                 for item in hooks.get(9 + full_blocks + 5 * g, []):
@@ -652,19 +665,17 @@
         sds = jax.ShapeDtypeStruct
         out_shape = [
             sds((n_l, n_c, 2 * NH, chunk, HD), BF), sds((n_l, 3, 2 * NH, chunk, HD), BF), sds((n_l, n_c, NH, chunk, HD), BF),
-            sds((n_l, n_c, 4, chunk, 5 * HD), BF), sds((n_l, n_c, 4, chunk, HD), BF), sds((n_l, n_c, chunk, dim), F32), sds((n_l, n_c, 2, unit, dim), BF),
-            sds((n_l, n_c, 2, 3, unit, dim), F32), sds((n_l, n_c, 2, 3, unit, dim), F32),
-            sds((n_l, n_c, 2, 2, unit, dim), F32), sds((n_l, n_c, 2, 2, unit, dim), F32),
-            sds((n_l, n_c, chunk, dim), BF), sds((n_l, 4 * local, dim), BF),
+            sds((n_l * n_c, 4, chunk, 3 * HD), BF), sds((n_l * n_c, 4, chunk, 2 * HD), BF), sds((n_l * n_c, chunk, dim), F32), sds((n_l * n_c * 2, unit, dim), BF),
+        ] + [sds((n_l * n_c * 6, unit, dim), F32)] * 4 + [
+            sds((n_l * n_c, chunk, dim), BF), sds((n_l, 4 * local, dim), BF),
         ] + [sds((n_resp, chunk, HD), F32)] * 3
-        gsem = lambda g: DMA((n_l, n_c) + g + (3, 2))
         outs = pl.pallas_call(
             functools.partial(program, (chunk, dim, hidden, vocab, HD ** -0.5)),
             out_shape=out_shape,
             in_specs=[ANY, ANY, VMEM, VMEM, VMEM, VMEM] + [ANY] * 10,
             out_specs=[ANY] * 13 + [VMEM] * 3,
-            scratch_shapes=[pltpu.VMEM((unit, dim), F32)] * 4 + [pltpu.VMEM((unit, dim), BF), DMA((4,))] + [gsem((1,))] * 2 + [gsem((2,))] * 4
-            + [DMA((n_l, 3))] * 2 + [DMA((n_l, 3, 2))] * 2 + [DMA((n_l, 7, 3))] * 2,
+            scratch_shapes=[pltpu.VMEM((unit, dim), F32)] * 4 + [pltpu.VMEM((unit, dim), BF), DMA((4,))] + [DMA((72,))] * 6
+            + [DMA((6,))] * 2 + [DMA((42,))] * 4,
             compiler_params=pltpu.CompilerParams(collective_id=0, has_side_effects=True, vmem_limit_bytes=67043328),
             name="decoder",
         )(x_prompt, x_resp, tgt, attn_gain, mlp_gain, final_gain[None], cos, sin, heads_first(w_query), heads_first(w_key), heads_first(w_value), w_out.reshape(n_l, local, dim), jnp.transpose(w_gate, (0, 2, 1)), jnp.transpose(w_up, (0, 2, 1)), w_down, w_vocab)

time: 912 us -> 877 us (0.962)
  the two profiles are of different devices: /device:TPU:7 before, /device:TPU:0 now
where the time goes in v3:
time: 877 us; the launch traced here: 867 us
  Pallas kernels  839 us (96%)
  blocking collectives  14.6 us (2%)
    pallas_call x1, Pallas kernels, device_step(): pl.pallas_call(functools.partial(program, (chunk, dim, hidden, vocab, HD...  839 us

profile of v3, /device:TPU:0, one launch (start us, length us, event | category | flops | bytes accessed | tf_op | source)
XLA Modules:
  0.0 866.8 jit_solution(8940224763304274579)
XLA Ops:
  0.1 2.8 fusion
  2.9 1.6 pad_maximum_fusion
  4.5 0.7 subtract_reduce_fusion
  5.2 1.1 sub.56.refs_2_
  6.3 1.3 broadcast_in_dim.6.refs_5_
  7.7 839.1 %decoder.1 = (bf16[2,3,10,512,128]{4,3,2,1,0:T(8,128)(2,1)}, bf16[2,3,10,512,128]{4,3,2,1,0:T(8,128)(2,1)}, bf16[2,3,5,512,128]{4,3,2,1,0:T(8,128)(2,1)}, bf16[6...) custom-call(bf16[512,2560]{1,0:T(8,128)(2,1)} %refs_0_.1, ...), custom_call_target="tpu_custom_call" | custom-call | tf_op jit(solution)/shard_map/decoder/pallas_call | solution.py:672
  846.8 1.3 slice_reduce_fusion.2
  848.0 1.3 slice_reduce_fusion.1
  849.3 1.3 slice_reduce_fusion
  850.6 14.6 %all-gather.1 = f32[4,3,1024]{2,1,0:T(4,128)S(1)} all-gather(f32[1,3,1024]{2,1,0:T(4,128)S(1)} %maximum_bitcast_fusion), channel_id=2, replica_groups=mesh['prompts'=2,'model'=4,'resp'=4] {'model'}, dimensions={0}, use_global_device_ids=true | all-gather | bytes 61440 | tf_op jit(solution)/shard_map/all_gather | solution.py:683
  865.2 0.1 slice_reduce_fusion.3
  866.0 0.6 compare_select_fusion
  (11 shorter events, 0.1 us)
